TPU v7x, 32 devices: a whole 2x2x4 slice. The times are simulated.
32 devices in a mesh: groups: 2 (over x), kvseq: 8 (over z, y), tensor: 2 (over core).
Axes of the slice: x: 2, y: 2, z: 4, core: 2. Of those that a mesh axis runs over, the one named last changes fastest.
Arguments:
- hidden: bfloat16 [16, 8192], P('groups', 'kvseq'), parts along dimension 0, may hold values from -30 to 30
- lengths: int32 [16], P('groups'), parts along dimension 0, may hold values from 128 to 2048, as said below
- key_cache: bfloat16 [16, 2048, 1024], P('groups', 'kvseq', 'tensor'), parts along dimension 0, may hold values from -400 to 400
- value_cache: bfloat16 [16, 2048, 1024], P('groups', 'kvseq', 'tensor'), parts along dimension 0, may hold values from -60 to 60
- gain_in: float32 [8192], P('kvseq'), may hold values from 0.1 to 1.9
- w_query: bfloat16 [8192, 8192], P('kvseq', 'tensor'), may hold values from -0.0625 to 0.0625
- w_key: bfloat16 [8192, 1024], P('kvseq', 'tensor'), may hold values from -0.0625 to 0.0625
- w_value: bfloat16 [8192, 1024], P('kvseq', 'tensor'), may hold values from -0.0625 to 0.0625
- w_output: bfloat16 [8192, 8192], P('tensor', 'kvseq'), may hold values from -0.0625 to 0.0625
- gain_post: float32 [8192], P('kvseq'), may hold values from 0.1 to 1.9
- w_gate: bfloat16 [8192, 15360], P('kvseq', 'tensor'), may hold values from -0.0625 to 0.0625
- w_up: bfloat16 [8192, 15360], P('kvseq', 'tensor'), may hold values from -0.0625 to 0.0625
- w_down: bfloat16 [15360, 8192], P('tensor', 'kvseq'), may hold values from -0.046875 to 0.046875
Outputs:
- output: bfloat16 [16, 8192], P('groups', 'kvseq'), parts along dimension 0
- new_keys: bfloat16 [16, 1024], P('groups', 'tensor'), parts along dimension 0
- new_values: bfloat16 [16, 1024], P('groups', 'tensor'), parts along dimension 0
There are 2 independent parts, one for each index of `groups`. A program takes and returns all parts, laid end to end along the dimension named above; an argument that names none is the same for every part. Nothing has to cross between parts.
Inputs may be any that keep to these rules, and one draw needn't show every extreme that they name: `lengths`: multiples of 128; some sequence holds exactly 2048.
All inputs are finite; a program needn't handle non-finite values.
Results may differ from a plain program's by a relative error of at most 0.024.
Values may be sent and summed in bfloat16 or wider, within the bound.
A program may use at most 128 MiB of HBM per device.

v0:
```python
import functools

import jax
import jax.numpy as jnp
import numpy as np
from jax import lax
from jax.experimental import pallas as pl
from jax.experimental.pallas import tpu as pltpu
from jax.sharding import PartitionSpec as P

HD = 128
epsilon = 1e-06
rope_base = 1000000.0
BF = jnp.bfloat16
F32 = jnp.float32
MESH = pl.DeviceIdType.MESH


def mult(x, m):
    return pl.multiple_of(x, m)


def when(cond, f):
    if cond is True:
        f()
    else:
        pl.when(cond)(f)


def split_kernel(packed, out, new_keys, new_values):
    Dl, KC = out.shape[1], new_keys.shape[1]
    out[...] = packed[:, :Dl]
    new_keys[...] = packed[:, Dl : Dl + KC]
    new_values[...] = packed[:, Dl + KC :]


def layer_kernel(
    c,
    lengths_hbm,
    hidden_hbm,
    gain_in_hbm,
    gain_post_hbm,
    freq_hbm,
    kc_hbm,
    vc_hbm,
    wq_hbm,
    wk_hbm,
    wv_hbm,
    wo_hbm,
    wg_hbm,
    wu_hbm,
    wd_hbm,
    out,
    lengths,
    hidden,
    gain_in,
    gain_post,
    freq,
    wqkv,
    tail,
    wo,
    wg,
    wu,
    kc,
    vc,
    early_a,
    send_a,
    recv_a,
    all_a,
    send_b,
    recv_b,
    send_m,
    recv_m,
    all_b,
    part_1,
    send_c,
    recv_c,
    all_c,
    part_2,
    wsem,
    fsem,
    dsem,
    sa_s,
    sa_r,
    ga_s,
    ga_r,
    sb_s,
    sb_r,
    sm_s,
    sm_r,
    gb_s,
    gb_r,
    t1_s,
    t1_r,
    sc_s,
    sc_r,
    gc_s,
    gc_r,
    t2_s,
    t2_r,
):
    n, T, A = c["n"], c["T"], c["A"]
    S, Dl, L = c["S"], c["Dl"], c["L"]
    QH, KH, W = c["QH"], c["KH"], c["W"]
    QC, KC = QH * HD, KH * HD
    TOT = QC + 2 * KC
    CA = TOT // A
    HA = CA // HD
    HB = QH // A
    CB = HB * HD
    FT = c["FT"]
    reuse = c["reuse"]
    per_group = QH // KH
    D = float(Dl * n)
    me = lax.axis_index("kvseq")
    t = lax.axis_index("tensor")
    owner = True if n == A else me < A

    def local(src, dst, sem):
        return pltpu.make_async_copy(src, dst, sem)

    half = Dl // 2
    first = [
        local(
            src.at[pl.ds(b * half, half), :],
            wqkv.at[pl.ds(b * half, half), pl.ds(at, width)],
            fsem.at[b * 3 + i],
        )
        for b in range(2)
        for i, (src, at, width) in enumerate(
            ((wq_hbm, 0, QC), (wk_hbm, QC, KC), (wv_hbm, QC + KC, KC))
        )
    ]
    later = [
        local(kc_hbm, kc, wsem.at[3]),
        local(vc_hbm, vc, wsem.at[4]),
        local(wo_hbm, wo, wsem.at[5]),
        local(wg_hbm, wg, wsem.at[6]),
        local(wu_hbm, wu, wsem.at[7]),
    ]

    def down_slot(d):
        return wqkv.at[:, pl.ds(d * Dl, Dl)] if d < reuse else tail.at[d - reuse]

    down = [
        local(wd_hbm.at[pl.ds((d * FT // A) * HD, W), :], down_slot(d), dsem.at[d])
        for d in range(A)
    ]
    small = [
        local(lengths_hbm, lengths, wsem.at[8]),
        local(hidden_hbm, hidden, wsem.at[9]),
        local(gain_in_hbm, gain_in, wsem.at[10]),
        local(gain_post_hbm, gain_post, wsem.at[11]),
        local(freq_hbm, freq, wsem.at[12]),
    ]
    for x in small + first:
        x.start()

    barrier = pltpu.get_barrier_semaphore()

    def greet(k, _):
        pl.semaphore_signal(
            barrier, inc=1, device_id={"kvseq": lax.rem(me + k, n)}, device_id_type=MESH
        )
        return 0

    lax.fori_loop(1, n, greet, 0)
    for k in range(1, T):
        pl.semaphore_signal(
            barrier, inc=1, device_id={"tensor": lax.rem(t + k, T)}, device_id_type=MESH
        )

    def remote(src, dst, s_sem, r_sem, to):
        return pltpu.make_async_remote_copy(
            src_ref=src, dst_ref=dst, send_sem=s_sem, recv_sem=r_sem, device_id=to,
            device_id_type=MESH,
        )

    def scatter(send, recv, s_sem, r_sem, d):
        return remote(send.at[d], recv.at[me], s_sem.at[d], r_sem.at[me], {"kvseq": d})

    def scatter_wait_recv(send, recv, s_sem, r_sem):
        def one(k, _):
            src = lax.rem(me + k, n)
            remote(
                send.at[0], recv.at[src], s_sem.at[0], r_sem.at[src], {"kvseq": src}
            ).wait_recv()
            return 0

        lax.fori_loop(1, n, one, 0)

    def scatter_wait_send(send, recv, s_sem, r_sem):
        for d in range(A):
            pl.when(d != me)(lambda d=d: scatter(send, recv, s_sem, r_sem, d).wait_send())

    def gather_start(view, s_sem, r_sem):
        def one(k, _):
            to = lax.rem(me + k, n)
            remote(view(me), view(me), s_sem.at[k], r_sem.at[me], {"kvseq": to}).start()
            return 0

        lax.fori_loop(1, n, one, 0)

    def gather_one(view, s_sem, r_sem, s):
        remote(view(s), view(s), s_sem.at[0], r_sem.at[s], {"kvseq": s}).wait_recv()

    def gather_wait_recv(view, s_sem, r_sem):
        def one(s, _):
            @pl.when(s != me)
            def _():
                remote(view(s), view(s), s_sem.at[0], r_sem.at[s], {"kvseq": s}).wait_recv()

            return 0

        lax.fori_loop(0, A, one, 0)

    def gather_wait_send(view, s_sem, r_sem):
        def one(k, _):
            to = lax.rem(me + k, n)
            remote(view(me), view(me), s_sem.at[k], r_sem.at[me], {"kvseq": to}).wait_send()
            return 0

        def run():
            lax.fori_loop(1, n, one, 0)

        when(owner, run)

    def pair_copies(part, s_sem, r_sem):
        return [
            remote(
                part.at[t], part.at[t], s_sem.at[k], r_sem.at[t], {"tensor": lax.rem(t + k, T)}
            )
            for k in range(1, T)
        ]

    def pair_sum(part, s_sem, r_sem):
        for x in pair_copies(part, s_sem, r_sem):
            x.start()
        for k in range(1, T):
            src = lax.rem(t + k, T)
            remote(
                part.at[src], part.at[src], s_sem.at[k], r_sem.at[src], {"tensor": src}
            ).wait_recv()
        total = part[0]
        for i in range(1, T):
            total = total + part[i]
        return total

    lane = lax.broadcasted_iota(jnp.int32, (S, HD), 1)
    row = lax.broadcasted_iota(jnp.int32, (S, HD), 0)

    def squares_block(x):
        s = jnp.broadcast_to(jnp.sum(x * x, axis=1, keepdims=True), (S, HD))
        high = s.astype(BF).astype(F32)
        return jnp.where(lane < HD // 2, high, s - high).astype(BF)

    def row_scale(block):
        total = jnp.sum(block, axis=1, keepdims=True) * (2.0 / HD)
        return lax.rsqrt(total / D + epsilon)

    def far_first(k):
        return lax.rem(me + A // 2 + ((k + 1) // 2) * (1 - 2 * (k % 2)) + A, A)

    def near_first(k):
        return far_first(A - 1 - k)

    for x in small:
        x.wait()
    stream = hidden[...].astype(F32)
    xg = (stream * gain_in[...]).astype(BF)
    sq = squares_block(stream)

    position = jnp.zeros((S, HD), F32)
    for s in range(S):
        position = jnp.where(row == s, lengths[s].astype(F32), position)
    angle = position * freq[...]
    cosine = jnp.cos(angle)
    sine = jnp.sin(angle)
    sine = jnp.where(lane < HD // 2, -sine, sine)

    for x in first[:3]:
        x.wait()
    def project_early(d, _):
        cols = pl.ds(mult(d * CA, HD), CA)
        early_a[d] = jnp.dot(xg[:, :half], wqkv[:half, cols], preferred_element_type=F32)
        return 0

    lax.fori_loop(0, A, project_early, 0)
    for x in first[3:]:
        x.wait()
    for x in later + down[reuse:]:
        x.start()
    pl.semaphore_wait(barrier, (n - 1) + (T - 1))

    def project(k, _):
        d = far_first(k)
        cols = pl.ds(mult(d * CA, HD), CA)
        part = early_a[d] + jnp.dot(
            xg[:, half:], wqkv[half:, cols], preferred_element_type=F32
        )
        send_a[d, :, :CA] = part.astype(BF)
        send_a[d, :, CA:] = sq

        @pl.when(d != me)
        def _():
            scatter(send_a, recv_a, sa_s, sa_r, d).start()

        return 0

    lax.fori_loop(0, A, project, 0)
    for x in down[:reuse]:
        x.start()

    def view_a(s):
        return all_a.at[:, pl.ds(mult(s * CA, HD), CA)]

    def reduce_a():
        recv_a[me] = send_a[me]
        scatter_wait_recv(send_a, recv_a, sa_s, sa_r)
        total = lax.fori_loop(
            1, n, lambda s, acc: acc + recv_a[s].astype(F32), recv_a[0].astype(F32)
        )
        scale = row_scale(total[:, CA:])
        for j in range(HA):
            v = total[:, j * HD : (j + 1) * HD] * scale
            turned = v * cosine + pltpu.roll(v, HD // 2, 1) * sine
            rot = jnp.broadcast_to(me * HA + j, (S, HD)) < QH + KH
            res = jnp.where(rot, turned, v).astype(BF)
            all_a[:, pl.ds(mult((me * HA + j) * HD, HD), HD)] = res
        gather_start(view_a, ga_s, ga_r)

    when(owner, reduce_a)
    gather_wait_recv(view_a, ga_s, ga_r)
    out[:, Dl:] = all_a[:, QC:]

    R = per_group * S
    brow = lax.broadcasted_iota(jnp.int32, (R, L), 0) % S
    orow = lax.broadcasted_iota(jnp.int32, (R, HD), 0) % S
    limit = jnp.zeros((R, L), jnp.int32)
    for s in range(S):
        limit = jnp.where(brow == s, lengths[s], limit)
    place = lax.broadcasted_iota(jnp.int32, (R, L), 1) + me * L
    valid = place < limit
    factor = float(HD) ** (-0.5)
    later[0].wait()
    later[1].wait()

    def attend(g, _):
        q = jnp.concatenate(
            [
                all_a[:, pl.ds(mult((g * per_group + j) * HD, HD), HD)].astype(F32)
                for j in range(per_group)
            ],
            axis=0,
        ).astype(BF)
        scores = jnp.zeros((R, L), F32)
        for s in range(S):
            keys = kc[s, :, pl.ds(mult(g * HD, HD), HD)]
            x = lax.dot_general(
                q, keys, (((1,), (1,)), ((), ())), preferred_element_type=F32
            )
            scores = jnp.where(brow == s, x, scores)
        scores = jnp.where(valid, scores * factor, -1e30)
        top = jnp.max(scores, axis=1, keepdims=True)
        w = jnp.where(valid, jnp.exp(scores - top), 0.0)
        total = jnp.sum(w, axis=1, keepdims=True)
        w = w.astype(BF)
        mixed = jnp.zeros((R, HD), F32)
        for s in range(S):
            vals = vc[s, :, pl.ds(mult(g * HD, HD), HD)]
            x = jnp.dot(w, vals, preferred_element_type=F32)
            mixed = jnp.where(orow == s, x, mixed)
        for i in range(per_group // HB):
            d = g * (per_group // HB) + i
            ml = jnp.zeros((S, HD), F32)
            for j in range(HB):
                r = (i * HB + j) * S
                send_b[d, :, j * HD : (j + 1) * HD] = mixed[r : r + S].astype(BF)
                ml = jnp.where(lane == j, top[r : r + S], ml)
                ml = jnp.where(lane == HD // 2 + j, total[r : r + S], ml)
            send_m[d] = ml

            @pl.when(d != me)
            def _():
                scatter(send_b, recv_b, sb_s, sb_r, d).start()
                scatter(send_m, recv_m, sm_s, sm_r, d).start()

        return 0

    lax.fori_loop(0, KH, attend, 0)

    def view_b(s):
        return all_b.at[:, pl.ds(mult(s * CB, HD), CB)]

    def reduce_b():
        recv_b[me] = send_b[me]
        recv_m[me] = send_m[me]
        scatter_wait_recv(send_m, recv_m, sm_s, sm_r)
        top = lax.fori_loop(1, n, lambda s, acc: jnp.maximum(acc, recv_m[s]), recv_m[0])
        scatter_wait_recv(send_b, recv_b, sb_s, sb_r)

        def join(s, state):
            total, mixed = state
            m = recv_m[s]
            scale = jnp.exp(m - top)
            total = total + pltpu.roll(m, HD // 2, 1) * scale
            x = recv_b[s].astype(F32)
            mixed = tuple(
                mixed[j] + x[:, j * HD : (j + 1) * HD] * scale[:, j : j + 1] for j in range(HB)
            )
            return total, mixed

        zero = jnp.zeros((S, HD), F32)
        total, mixed = lax.fori_loop(0, n, join, (zero, (zero,) * HB))
        for j in range(HB):
            h = me * HB + j
            g = h // per_group
            q = all_a[:, pl.ds(mult(h * HD, HD), HD)].astype(F32)
            key = all_a[:, pl.ds(mult(QC + g * HD, HD), HD)].astype(F32)
            val = all_a[:, pl.ds(mult(QC + KC + g * HD, HD), HD)].astype(F32)
            own = jnp.sum(q * key, axis=1, keepdims=True) * factor
            old = top[:, j : j + 1]
            best = jnp.maximum(old, own)
            old_scale = jnp.exp(old - best)
            own_weight = jnp.exp(own - best)
            bottom = total[:, j : j + 1] * old_scale + own_weight
            res = (mixed[j] * old_scale + own_weight * val) / bottom
            all_b[:, pl.ds(mult(h * HD, HD), HD)] = res.astype(BF)
        gather_start(view_b, gb_s, gb_r)

    when(owner, reduce_b)
    later[2].wait()
    part_1[t] = jnp.zeros((S, Dl), F32)

    def output_block(k, _):
        d = near_first(k)

        @pl.when(d != me)
        def _():
            gather_one(view_b, gb_s, gb_r, d)

        x = all_b[:, pl.ds(mult(d * CB, HD), CB)]
        part_1[t] += jnp.dot(x, wo[pl.ds(mult(d * CB, HD), CB), :], preferred_element_type=F32)
        return 0

    lax.fori_loop(0, A, output_block, 0)
    residual = hidden[...].astype(F32) + pair_sum(part_1, t1_s, t1_r)
    sq_post = squares_block(residual)
    rg = (residual * gain_post[...]).astype(BF)
    later[3].wait()
    later[4].wait()

    def widen(k, _):
        d = far_first(k)
        begin = (d * FT // A) * HD
        for i, w in enumerate((wg, wu)):
            for j in range(0, W, 256):
                step = min(256, W - j)
                x = jnp.dot(
                    rg, w[:, pl.ds(mult(begin + j, HD), step)], preferred_element_type=F32
                )
                send_c[d, :, i * W + j : i * W + j + step] = x.astype(BF)
        send_c[d, :, 2 * W :] = sq_post

        @pl.when(d != me)
        def _():
            scatter(send_c, recv_c, sc_s, sc_r, d).start()

        return 0

    lax.fori_loop(0, A, widen, 0)

    def view_c(s):
        return all_c.at[s]

    def reduce_c():
        recv_c[me] = send_c[me]
        scatter_wait_recv(send_c, recv_c, sc_s, sc_r)
        total = lax.fori_loop(
            1, n, lambda s, acc: acc + recv_c[s].astype(F32), recv_c[0].astype(F32)
        )
        scale = row_scale(total[:, 2 * W :])
        gate = total[:, :W] * scale
        up = total[:, W : 2 * W] * scale
        inner = gate * jax.nn.sigmoid(gate) * up
        owned = ((me + 1) * FT // A - me * FT // A) * HD
        col = lax.broadcasted_iota(jnp.int32, (S, W), 1)
        all_c[me] = jnp.where(col < owned, inner, 0.0).astype(BF)
        gather_start(view_c, gc_s, gc_r)

    when(owner, reduce_c)
    for x in down:
        x.wait()
    part_2[t] = jnp.zeros((S, Dl), F32)

    def down_block(k, _):
        d = near_first(k)

        @pl.when(d != me)
        def _():
            gather_one(view_c, gc_s, gc_r, d)

        x = all_c[d]
        if reuse:

            @pl.when(d < reuse)
            def _():
                w = wqkv[:, pl.ds(mult(d * Dl, HD), Dl)]
                part_2[t] += jnp.dot(x, w, preferred_element_type=F32)

        if reuse < A:

            @pl.when(d >= reuse)
            def _():
                w = tail[jnp.maximum(d - reuse, 0)]
                part_2[t] += jnp.dot(x, w, preferred_element_type=F32)

        return 0

    lax.fori_loop(0, A, down_block, 0)
    out[:, :Dl] = (residual + pair_sum(part_2, t2_s, t2_r)).astype(BF)

    scatter_wait_send(send_a, recv_a, sa_s, sa_r)
    gather_wait_send(view_a, ga_s, ga_r)
    scatter_wait_send(send_b, recv_b, sb_s, sb_r)
    scatter_wait_send(send_m, recv_m, sm_s, sm_r)
    gather_wait_send(view_b, gb_s, gb_r)
    scatter_wait_send(send_c, recv_c, sc_s, sc_r)
    gather_wait_send(view_c, gc_s, gc_r)
    for part, s_sem, r_sem in ((part_1, t1_s, t1_r), (part_2, t2_s, t2_r)):
        for x in pair_copies(part, s_sem, r_sem):
            x.wait_send()


def per_device(
    n,
    T,
    hidden,
    lengths,
    key_cache,
    value_cache,
    gain_in,
    w_query,
    w_key,
    w_value,
    w_output,
    gain_post,
    w_gate,
    w_up,
    w_down,
):
    S, Dl = hidden.shape
    L = key_cache.shape[1]
    QC, KC = w_query.shape[1], w_key.shape[1]
    QH, KH = QC // HD, KC // HD
    FT = w_gate.shape[1] // HD
    A = max(
        a
        for a in range(1, n + 1)
        if n % a == 0
        and (QH + 2 * KH) % a == 0
        and QH % a == 0
        and (QH // KH) % (QH // a) == 0
        and a <= FT
    )
    W = -(-FT // A) * HD
    TOT = QC + 2 * KC
    reuse = min(A, TOT // Dl) if Dl == W else 0
    c = dict(n=n, T=T, A=A, S=S, Dl=Dl, L=L, QH=QH, KH=KH, W=W, FT=FT, reuse=reuse)
    CA, CB = TOT // A, QC // A
    CC = 2 * W + HD
    half = np.arange(HD) % (HD // 2)
    freq = jnp.asarray((rope_base ** (-half * 2.0 / HD)).astype(np.float32)[None, :])
    dma = pltpu.SemaphoreType.DMA
    V = pltpu.VMEM
    anywhere = pl.BlockSpec(memory_space=pl.ANY)
    vmem = pl.BlockSpec(memory_space=pltpu.VMEM)
    packed = pl.pallas_call(
        functools.partial(layer_kernel, c),
        out_shape=jax.ShapeDtypeStruct((S, Dl + 2 * KC), BF),
        in_specs=[anywhere] * 14,
        out_specs=vmem,
        scratch_shapes=[
            pltpu.SMEM(lengths.shape, jnp.int32),
            V((S, Dl), BF),
            V((1, Dl), F32),
            V((1, Dl), F32),
            V((1, HD), F32),
            V((Dl, TOT), BF),
            V((max(A - reuse, 1), W, Dl), BF),
            V((QC, Dl), BF),
            V((Dl, FT * HD), BF),
            V((Dl, FT * HD), BF),
            V(key_cache.shape, BF),
            V(value_cache.shape, BF),
            V((A, S, CA), F32),
            V((A, S, CA + HD), BF),
            V((n, S, CA + HD), BF),
            V((S, TOT), BF),
            V((A, S, CB), BF),
            V((n, S, CB), BF),
            V((A, S, HD), F32),
            V((n, S, HD), F32),
            V((S, QC), BF),
            V((T, S, Dl), F32),
            V((A, S, CC), BF),
            V((n, S, CC), BF),
            V((A, S, W), BF),
            V((T, S, Dl), F32),
            dma((13,)),
            dma((6,)),
            dma((A,)),
            dma((A,)),
            dma((n,)),
            dma((n,)),
            dma((A,)),
            dma((A,)),
            dma((n,)),
            dma((A,)),
            dma((n,)),
            dma((n,)),
            dma((A,)),
            dma((T,)),
            dma((T,)),
            dma((A,)),
            dma((n,)),
            dma((n,)),
            dma((A,)),
            dma((T,)),
            dma((T,)),
        ],
        compiler_params=pltpu.CompilerParams(
            collective_id=0, has_side_effects=True, vmem_limit_bytes=67000000
        ),
    )(
        lengths,
        hidden,
        gain_in[None, :],
        gain_post[None, :],
        freq,
        key_cache,
        value_cache,
        w_query,
        w_key,
        w_value,
        w_output,
        w_gate,
        w_up,
        w_down,
    )
    return pl.pallas_call(
        split_kernel,
        out_shape=(
            jax.ShapeDtypeStruct((S, Dl), BF),
            jax.ShapeDtypeStruct((S, KC), BF),
            jax.ShapeDtypeStruct((S, KC), BF),
        ),
        in_specs=[vmem],
        out_specs=(vmem,) * 3,
    )(packed)


def solution(mesh):
    placed = (
        P("groups", "kvseq"),
        P("groups"),
        P("groups", "kvseq", "tensor"),
        P("groups", "kvseq", "tensor"),
        P("kvseq"),
        P("kvseq", "tensor"),
        P("kvseq", "tensor"),
        P("kvseq", "tensor"),
        P("tensor", "kvseq"),
        P("kvseq"),
        P("kvseq", "tensor"),
        P("kvseq", "tensor"),
        P("tensor", "kvseq"),
    )
    return jax.shard_map(
        functools.partial(per_device, mesh.shape["kvseq"], mesh.shape["tensor"]),
        mesh=mesh,
        in_specs=placed,
        out_specs=(P("groups", "kvseq"), P("groups", "tensor"), P("groups", "tensor")),
        check_vma=False,
    )
```

profile of v0, /device:TPU:0, one launch (start us, length us, event | category | flops | bytes accessed | tf_op | source)
XLA Modules:
  0.0 51.7 jit_solution(7633281373908146659)
XLA Ops:
  0.6 49.6 %shard_map.157.packed = bf16[8,2048]{1,0:T(8,128)(2,1)} custom-call(s32[8]{0:T(128)} %lengths_hbm.1, bf16[8,1024]{1,0:T(8,128)(2,1)} %hidden_hbm.1, f32[1,1024]{1,0:T(1,128)} %bitcast.2, f32[1,1024]{1,0:T(1,128)} %bitcast.3, f32[1,128]{1,0:T(1,128)} %constant.2.clone.freq_hbm, bf16[8,256,512]{2,1,0:T(8,128)(2,1)} %kc_hbm.1, bf16[8,256,512]{2,1,0:T(8,128)(2,1)} %vc_hbm.1, ...), custom_call_target="tpu_custom_call" | custom-call | tf_op jit(solution)/shard_map/pallas_call | solution.py:578
  50.3 1.4 %shard_map.158 = (bf16[8,1024]{1,0:T(8,128)(2,1)}, bf16[8,512]{1,0:T(8,128)(2,1)}, bf16[8,512]{1,0:T(8,128)(2,1)}) custom-call(bf16[8,2048]{1,0:T(8,128)(2,1)} %shard_map.157.packed), custom_call_target="tpu_custom_call" | custom-call | tf_op jit(solution)/shard_map/pallas_call | solution.py:651
where the time goes:
time: 51.9 us; the launch traced here: 51.7 us
  Pallas kernels  51 us (98%)
  between operations  0.64 us (1%)
    pallas_call x1, Pallas kernels, per_device(): pl.pallas_call(functools.partial(layer_kernel, c), out_shape=jax.ShapeDty...  49.6 us
    pallas_call x1, Pallas kernels, per_device(): pl.pallas_call(split_kernel, out_shape=(jax.ShapeDtypeStruct((S, Dl), BF)...  1.37 us

commit v1 on v0

v1 whole, which is shorter than its diff:
```python
import functools

import jax
import jax.numpy as jnp
import numpy as np
from jax import lax
from jax.experimental import pallas as pl
from jax.experimental.pallas import tpu as pltpu
from jax.sharding import PartitionSpec as P

HD = 128
epsilon = 1e-06
rope_base = 1000000.0
BF = jnp.bfloat16
F32 = jnp.float32
MESH = pl.DeviceIdType.MESH


def mult(x, m):
    return pl.multiple_of(x, m)


def accumulate(n, load, op=jnp.add):
    u = 8 if n % 8 == 0 else 1

    def group(first, acc):
        for j in range(u):
            x = load(first + j)
            acc = x if acc is None else jax.tree.map(op, acc, x)
        return acc

    acc = group(0, None)
    if n == u:
        return acc
    return lax.fori_loop(1, n // u, lambda i, a: group(i * u, a), acc)


def split_kernel(packed, out, new_keys, new_values):
    Dl, KC = out.shape[1], new_keys.shape[1]
    out[...] = packed[:, :Dl]
    new_keys[...] = packed[:, Dl : Dl + KC]
    new_values[...] = packed[:, Dl + KC :]


def layer_kernel(
    c,
    lengths_hbm,
    hidden_hbm,
    gain_in_hbm,
    gain_post_hbm,
    freq_hbm,
    kc_hbm,
    vc_hbm,
    wq_hbm,
    wk_hbm,
    wv_hbm,
    wo_hbm,
    wg_hbm,
    wu_hbm,
    wd_hbm,
    out,
    lengths,
    hidden,
    gain_in,
    gain_post,
    freq,
    wqkv,
    tail,
    wo,
    wg,
    wu,
    kc,
    vc,
    send_a,
    recv_a,
    qg,
    kvg,
    own_scores,
    all_q,
    all_kv,
    send_b,
    recv_b,
    ab,
    all_b,
    part_1,
    send_c0,
    send_c1,
    recv_c0,
    recv_c1,
    ic0,
    ic1,
    all_c0,
    all_c1,
    part_2,
    ssem,
    wsem,
    fsem,
    dsem,
    sa_s,
    sa_r,
    ga_s,
    ga_r,
    gk_s,
    gk_r,
    sb_s,
    sb_r,
    gb_s,
    gb_r,
    t1_s,
    t1_r,
    sc_s,
    sc_r,
    gc_s,
    gc_r,
    t2_s,
    t2_r,
):
    n, T, O = c["n"], c["T"], c["O"]
    S, Dl, L = c["S"], c["Dl"], c["L"]
    PG, FO, F0, F1 = c["PG"], c["FO"], c["F0"], c["F1"]
    QG = PG * HD
    G3 = QG + 2 * HD
    KC = O * HD
    W0, W1 = F0 * HD, F1 * HD
    D = float(Dl * n)
    base = (n - O) // 2
    me = lax.axis_index("kvseq")
    t = lax.axis_index("tensor")
    owner = (me >= base) & (me < base + O) & (t == T - 1)
    o_me = me - base
    half_n = n // 2
    side = me // half_n

    def mine(o):
        return (me == base + o) & (t == T - 1)

    def order(k):
        if O != 4:
            return lax.rem(me + k, O)
        oz = (side + 1 + k // 2) % 2
        oy = (me + 1 + k % 2) % 2
        return oz * 2 + oy

    def near(k):
        return order(O - 1 - k)

    def local(src, dst, sem):
        return pltpu.make_async_copy(src, dst, sem)

    small = [
        local(hidden_hbm, hidden, ssem.at[0]),
        local(gain_in_hbm, gain_in, ssem.at[1]),
        local(lengths_hbm, lengths, ssem.at[2]),
        local(freq_hbm, freq, ssem.at[3]),
        local(gain_post_hbm, gain_post, ssem.at[4]),
    ]
    half = Dl // 2

    def first(k):
        o = order(k)
        return [
            [
                local(
                    src.at[pl.ds(b * half, half), pl.ds(mult(o * width, HD), width)],
                    wqkv.at[k, pl.ds(b * half, half), pl.ds(at, width)],
                    fsem.at[k, b, i],
                )
                for i, (src, at, width) in enumerate(
                    ((wq_hbm, 0, QG), (wk_hbm, QG, HD), (wv_hbm, QG + HD, HD))
                )
            ]
            for b in range(2)
        ]

    firsts = [first(k) for k in range(O)]
    kv_copies = [local(kc_hbm, kc, wsem.at[0]), local(vc_hbm, vc, wsem.at[1])]
    later = [
        local(wo_hbm, wo, wsem.at[2]),
        local(wg_hbm, wg, wsem.at[3]),
        local(wu_hbm, wu, wsem.at[4]),
    ]

    def down_0(o):
        return wo.at[pl.ds(mult(o * QG, HD), W0), :]

    def down_1(o):
        return wqkv.at[o, pl.ds(0, W1), pl.ds(0, Dl)] if c["reuse"] else tail.at[o]

    downs_0 = [
        local(wd_hbm.at[pl.ds(o * FO * HD, W0), :], down_0(o), dsem.at[0, o]) for o in range(O)
    ]
    downs_1 = [
        local(wd_hbm.at[pl.ds((o * FO + F0) * HD, W1), :], down_1(o), dsem.at[1, o])
        for o in range(O)
    ]
    for x in small:
        x.start()
    for k in range(O):
        for b in range(2):
            for x in firsts[k][b]:
                x.start(priority=1)

    barrier = pltpu.get_barrier_semaphore()
    for dt in range(T):

        def greet(k, _):
            pl.semaphore_signal(
                barrier,
                inc=1,
                device_id={"kvseq": lax.rem(me + k, n), "tensor": lax.rem(t + dt, T)},
                device_id_type=MESH,
            )
            return 0

        lax.fori_loop(0 if dt else 1, n, greet, 0)

    def remote(src, dst, s_sem, r_sem, k, tt):
        return pltpu.make_async_remote_copy(
            src_ref=src, dst_ref=dst, send_sem=s_sem, recv_sem=r_sem,
            device_id={"kvseq": k, "tensor": tt}, device_id_type=MESH,
        )

    def to_owner(src, recv, s_sem, r_sem, o):
        return remote(src, recv, s_sem, r_sem, base + o, T - 1)

    def scatter(src, dst, s_sem, r_sem, o):
        @pl.when(jnp.logical_not(mine(o)))
        def _():
            to_owner(src, dst, s_sem, r_sem, o).start()

        @pl.when(mine(o))
        def _():
            dst[...] = src[...]

    def scatter_wait_send(src, dst, s_sem, r_sem, o):
        @pl.when(jnp.logical_not(mine(o)))
        def _():
            to_owner(src, dst, s_sem, r_sem, o).wait_send()

    def owner_wait(recv, s_sem, r_sem, tt):
        def one(k, _):
            def wait():
                remote(recv(k), recv(k), s_sem, r_sem(k), k, tt).wait_recv()

            if tt == T - 1:
                pl.when(k != me)(wait)
            else:
                wait()
            return 0

        lax.fori_loop(0, n, one, 0)

    def each_target(f):
        def cross(k, _):
            f(k + (1 - side) * (n - 1 - 2 * k))
            return 0

        def same(k, _):
            f(k + side * (n - 1 - 2 * k))
            return 0

        lax.fori_loop(0, half_n, cross, 0)
        lax.fori_loop(0, n - half_n, same, 0)

    def spread(src, dst, s_sem, r_sem, tt):
        def one(d):
            def send():
                remote(src, dst, s_sem.at[tt, d], r_sem, d, tt).start()

            if tt == T - 1:
                pl.when(d != me)(send)
            else:
                send()

        each_target(one)
        if tt == T - 1:
            dst[...] = src[...]

    def spread_wait_send(src, dst, s_sem, r_sem, tt):
        def one(d, _):
            def wait():
                remote(src, dst, s_sem.at[tt, d], r_sem, d, tt).wait_send()

            if tt == T - 1:
                pl.when(d != me)(wait)
            else:
                wait()
            return 0

        lax.fori_loop(0, n, one, 0)

    def spread_wait(dst, s_sem, r_sem, o):
        @pl.when(jnp.logical_not(mine(o)))
        def _():
            remote(dst, dst, s_sem.at[0, 0], r_sem, base + o, T - 1).wait_recv()

    def pair_copies(part, s_sem, r_sem):
        return [
            remote(part.at[t], part.at[t], s_sem.at[k], r_sem.at[t], me, lax.rem(t + k, T))
            for k in range(1, T)
        ]

    def pair_sum(part, s_sem, r_sem):
        for x in pair_copies(part, s_sem, r_sem):
            x.start()
        for k in range(1, T):
            src = lax.rem(t + k, T)
            remote(part.at[src], part.at[src], s_sem.at[k], r_sem.at[src], me, src).wait_recv()
        total = part[0]
        for i in range(1, T):
            total = total + part[i]
        return total

    lane = lax.broadcasted_iota(jnp.int32, (S, HD), 1)
    row = lax.broadcasted_iota(jnp.int32, (S, HD), 0)

    def squares_block(x):
        s = jnp.broadcast_to(jnp.sum(x * x, axis=1, keepdims=True), (S, HD))
        high = s.astype(BF).astype(F32)
        return jnp.where(lane < HD // 2, high, s - high).astype(BF)

    def row_scale(block):
        total = jnp.sum(block, axis=1, keepdims=True) * (2.0 / HD)
        return lax.rsqrt(total / D + epsilon)

    small[0].wait()
    small[1].wait()
    stream = hidden[...].astype(F32)
    xg = (stream * gain_in[...]).astype(BF)
    sq = squares_block(stream)

    for k in range(O):
        o = order(k)
        for x in firsts[k][0]:
            x.wait()
        part = jnp.dot(xg[:, :half], wqkv[k, :half, :], preferred_element_type=F32)
        for x in firsts[k][1]:
            x.wait()
        if k == max(O - 2, 0):
            for x in kv_copies:
                x.start(priority=1)
        part = part + jnp.dot(xg[:, half:], wqkv[k, half:, :], preferred_element_type=F32)
        send_a[k, :, :G3] = part.astype(BF)
        send_a[k, :, G3:] = sq
        if k == 0:
            pl.semaphore_wait(barrier, n * T - 1)
        scatter(send_a.at[k], recv_a.at[t, me], sa_s.at[k], sa_r.at[t, me], o)
    for x in later + downs_1:
        x.start(priority=1)

    small[2].wait()
    small[3].wait()
    position = jnp.zeros((S, HD), F32)
    for s in range(S):
        position = jnp.where(row == s, lengths[s].astype(F32), position)
    angle = position * freq[...]
    cosine = jnp.cos(angle)
    sine = jnp.sin(angle)
    sine = jnp.where(lane < HD // 2, -sine, sine)
    factor = float(HD) ** (-0.5)

    @pl.when(owner)
    def _():
        for tt in reversed(range(T)):
            owner_wait(lambda k: recv_a.at[tt, k], sa_s.at[0], lambda k: sa_r.at[tt, k], tt)
            total = accumulate(n, lambda k: recv_a[tt, k].astype(F32))
            scale = row_scale(total[:, G3:])
            for j in range(PG + 1):
                v = total[:, j * HD : (j + 1) * HD] * scale
                v = (v * cosine + pltpu.roll(v, HD // 2, 1) * sine).astype(BF)
                if j < PG:
                    qg[tt, :, j * HD : (j + 1) * HD] = v
                else:
                    kvg[tt, :, :HD] = v
            kvg[tt, :, HD:] = (total[:, QG + HD : G3] * scale).astype(BF)
            spread(qg.at[tt], all_q.at[o_me], ga_s, ga_r.at[o_me], tt)
        for tt in range(T):
            spread(kvg.at[tt], all_kv.at[o_me], gk_s, gk_r.at[o_me], tt)
        for tt in range(T):
            key = kvg[tt, :, :HD].astype(F32)
            block = jnp.zeros((S, HD), F32)
            for j in range(PG):
                q = qg[tt, :, j * HD : (j + 1) * HD].astype(F32)
                block = jnp.where(
                    lane == j, jnp.sum(q * key, axis=1, keepdims=True) * factor, block
                )
            own_scores[tt] = block

    R = PG * S
    brow = lax.broadcasted_iota(jnp.int32, (R, L), 0) % S
    orow = lax.broadcasted_iota(jnp.int32, (R, HD), 0) % S
    limit = jnp.zeros((R, L), jnp.int32)
    for s in range(S):
        limit = jnp.where(brow == s, lengths[s], limit)
    place = lax.broadcasted_iota(jnp.int32, (R, L), 1) + me * L
    valid = place < limit
    for x in kv_copies:
        x.wait()
    group = lane % 16
    third = (lane % (HD // 2)) // 16

    def attend(i, _):
        g = near(i)
        spread_wait(all_q.at[g], ga_s, ga_r.at[g], g)
        q = jnp.concatenate(
            [all_q[g, :, j * HD : (j + 1) * HD].astype(F32) for j in range(PG)], axis=0
        ).astype(BF)
        cols = pl.ds(mult(g * HD, HD), HD)
        scores = jnp.zeros((R, L), F32)
        for s in range(S):
            x = lax.dot_general(
                q, kc[s, :, cols], (((1,), (1,)), ((), ())), preferred_element_type=F32
            )
            scores = jnp.where(brow == s, x, scores)
        scores = jnp.where(valid, scores * factor, -1e30)
        top = jnp.max(scores, axis=1, keepdims=True)
        w = jnp.where(valid, jnp.exp(scores - top), 0.0)
        total = jnp.sum(w, axis=1, keepdims=True)
        w = w.astype(BF)
        mixed = jnp.zeros((R, HD), F32)
        for s in range(S):
            x = jnp.dot(w, vc[s, :, cols], preferred_element_type=F32)
            mixed = jnp.where(orow == s, x, mixed)
        ml = jnp.zeros((S, HD), F32)
        for j in range(PG):
            rows = slice(j * S, (j + 1) * S)
            send_b[g, :, j * HD : (j + 1) * HD] = mixed[rows].astype(BF)
            ml = jnp.where(group == j, jnp.where(lane < HD // 2, top[rows], total[rows]), ml)
        high = ml.astype(BF).astype(F32)
        rest = ml - high
        middle = rest.astype(BF).astype(F32)
        low = rest - middle
        parts = jnp.where(third == 0, high, jnp.where(third == 1, middle, low))
        send_b[g, :, QG:] = parts.astype(BF)
        scatter(send_b.at[g], recv_b.at[t, me], sb_s.at[g], sb_r.at[t, me], g)
        return 0

    lax.fori_loop(0, O, attend, 0)

    @pl.when(owner)
    def _():
        for tt in reversed(range(T)):
            owner_wait(lambda k: recv_b.at[tt, k], sb_s.at[0], lambda k: sb_r.at[tt, k], tt)

            def stats(k):
                x = recv_b[tt, k, :, QG:].astype(F32)
                return x + pltpu.roll(x, HD - 16, 1) + pltpu.roll(x, HD - 32, 1)

            top = accumulate(n, stats, jnp.maximum)
            total = accumulate(
                n, lambda k: pltpu.roll(stats(k), HD // 2, 1) * jnp.exp(stats(k) - top)
            )
            own = own_scores[tt]
            best = jnp.maximum(top, own)
            old_scale = jnp.exp(top - best)
            own_weight = jnp.exp(own - best)
            bottom = total * old_scale + own_weight
            old_scale = old_scale / bottom
            own_weight = own_weight / bottom

            def weighted(k):
                scale = jnp.exp(stats(k) - top) * old_scale
                return tuple(
                    recv_b[tt, k, :, j * HD : (j + 1) * HD].astype(F32) * scale[:, j : j + 1]
                    for j in range(PG)
                )

            mixed = accumulate(n, weighted)
            val = kvg[tt, :, HD:].astype(F32)
            for j in range(PG):
                res = mixed[j] + own_weight[:, j : j + 1] * val
                ab[tt, :, j * HD : (j + 1) * HD] = res.astype(BF)
            spread(ab.at[tt], all_b.at[o_me], gb_s, gb_r.at[o_me], tt)

    later[0].wait()

    def output_block(i, acc):
        g = near(i)
        spread_wait(all_b.at[g], gb_s, gb_r.at[g], g)
        w = wo[pl.ds(mult(g * QG, HD), QG), :]
        return acc + jnp.dot(all_b[g], w, preferred_element_type=F32)

    part_1[t] = lax.fori_loop(0, O, output_block, jnp.zeros((S, Dl), F32))
    for x in downs_0:
        x.start(priority=1)
    small[4].wait()
    residual = hidden[...].astype(F32) + pair_sum(part_1, t1_s, t1_r)
    sq_post = squares_block(residual)
    rg = (residual * gain_post[...]).astype(BF)
    later[1].wait()
    later[2].wait()

    def widen(k, _):
        o = order(k)
        for send, recv, i, at, W in (
            (send_c0, recv_c0, 0, 0, W0),
            (send_c1, recv_c1, 1, F0, W1),
        ):
            begin = (o * FO + at) * HD
            for b, w in enumerate((wg, wu)):
                for j in range(0, W, 256):
                    step = min(256, W - j)
                    x = jnp.dot(
                        rg, w[:, pl.ds(mult(begin + j, HD), step)], preferred_element_type=F32
                    )
                    send[o, :, b * W + j : b * W + j + step] = x.astype(BF)
            if i == 0:
                send[o, :, 2 * W :] = sq_post
            scatter(send.at[o], recv.at[t, me], sc_s.at[o, i], sc_r.at[t, me, i], o)
        return 0

    lax.fori_loop(0, O, widen, 0)

    for g in range(O):
        spread_wait(all_kv.at[g], gk_s, gk_r.at[g], g)
        out[:, Dl + g * HD : Dl + (g + 1) * HD] = all_kv[g, :, :HD]
        out[:, Dl + KC + g * HD : Dl + KC + (g + 1) * HD] = all_kv[g, :, HD:]

    @pl.when(owner)
    def _():
        scales = [None] * T
        for i, recv, ic, all_c, W in ((0, recv_c0, ic0, all_c0, W0), (1, recv_c1, ic1, all_c1, W1)):
            for tt in reversed(range(T)):
                owner_wait(
                    lambda k: recv.at[tt, k], sc_s.at[0, 0], lambda k: sc_r.at[tt, k, i], tt
                )
                if i == 0:
                    scales[tt] = row_scale(
                        accumulate(n, lambda k: recv[tt, k, :, 2 * W :].astype(F32))
                    )
                for j in range(0, W, HD):
                    gate = accumulate(n, lambda k: recv[tt, k, :, j : j + HD].astype(F32))
                    up = accumulate(n, lambda k: recv[tt, k, :, W + j : W + j + HD].astype(F32))
                    gate = gate * scales[tt]
                    up = up * scales[tt]
                    ic[tt, :, j : j + HD] = (gate * jax.nn.sigmoid(gate) * up).astype(BF)
                spread(ic.at[tt], all_c.at[o_me], gc_s.at[i], gc_r.at[o_me, i], tt)

    for x in downs_0 + downs_1:
        x.wait()

    def down_block(k, acc):
        o = near(k)
        spread_wait(all_c0.at[o], gc_s.at[0], gc_r.at[o, 0], o)
        acc = acc + jnp.dot(all_c0[o], down_0(o)[...], preferred_element_type=F32)
        spread_wait(all_c1.at[o], gc_s.at[1], gc_r.at[o, 1], o)
        return acc + jnp.dot(all_c1[o], down_1(o)[...], preferred_element_type=F32)

    part_2[t] = lax.fori_loop(0, O, down_block, jnp.zeros((S, Dl), F32))
    out[:, :Dl] = (residual + pair_sum(part_2, t2_s, t2_r)).astype(BF)

    for k in range(O):
        scatter_wait_send(send_a.at[k], recv_a.at[t, me], sa_s.at[k], sa_r.at[t, me], order(k))

    def sent(o, _):
        scatter_wait_send(send_b.at[o], recv_b.at[t, me], sb_s.at[o], sb_r.at[t, me], o)
        for i, send, recv in ((0, send_c0, recv_c0), (1, send_c1, recv_c1)):
            scatter_wait_send(
                send.at[o], recv.at[t, me], sc_s.at[o, i], sc_r.at[t, me, i], o
            )
        return 0

    lax.fori_loop(0, O, sent, 0)

    @pl.when(owner)
    def _():
        for tt in range(T):
            spread_wait_send(qg.at[tt], all_q.at[o_me], ga_s, ga_r.at[o_me], tt)
            spread_wait_send(kvg.at[tt], all_kv.at[o_me], gk_s, gk_r.at[o_me], tt)
            spread_wait_send(ab.at[tt], all_b.at[o_me], gb_s, gb_r.at[o_me], tt)
            spread_wait_send(ic0.at[tt], all_c0.at[o_me], gc_s.at[0], gc_r.at[o_me, 0], tt)
            spread_wait_send(ic1.at[tt], all_c1.at[o_me], gc_s.at[1], gc_r.at[o_me, 1], tt)

    for part, s_sem, r_sem in ((part_1, t1_s, t1_r), (part_2, t2_s, t2_r)):
        for x in pair_copies(part, s_sem, r_sem):
            x.wait_send()


def per_device(
    n,
    T,
    hidden,
    lengths,
    key_cache,
    value_cache,
    gain_in,
    w_query,
    w_key,
    w_value,
    w_output,
    gain_post,
    w_gate,
    w_up,
    w_down,
):
    S, Dl = hidden.shape
    L = key_cache.shape[1]
    QC, KC = w_query.shape[1], w_key.shape[1]
    O = KC // HD
    PG = QC // KC
    FT = w_gate.shape[1] // HD
    assert n >= O and n % 2 == 0 and FT % O == 0 and PG <= 16
    FO = FT // O
    F0 = FO // 2
    F1 = FO - F0
    QG = PG * HD
    G3 = QG + 2 * HD
    W0, W1 = F0 * HD, F1 * HD
    assert W0 <= QG
    reuse = W1 <= Dl <= G3
    c = dict(n=n, T=T, O=O, S=S, Dl=Dl, L=L, PG=PG, FO=FO, F0=F0, F1=F1, reuse=reuse)
    half = np.arange(HD) % (HD // 2)
    freq = jnp.asarray((rope_base ** (-half * 2.0 / HD)).astype(np.float32)[None, :])
    dma = pltpu.SemaphoreType.DMA
    V = pltpu.VMEM
    anywhere = pl.BlockSpec(memory_space=pl.ANY)
    vmem = pl.BlockSpec(memory_space=pltpu.VMEM)
    packed = pl.pallas_call(
        functools.partial(layer_kernel, c),
        out_shape=jax.ShapeDtypeStruct((S, Dl + 2 * KC), BF),
        in_specs=[anywhere] * 14,
        out_specs=vmem,
        scratch_shapes=[
            pltpu.SMEM(lengths.shape, jnp.int32),
            V((S, Dl), BF),
            V((1, Dl), F32),
            V((1, Dl), F32),
            V((1, HD), F32),
            V((O, Dl, G3), BF),
            V((1, 16, HD) if reuse else (O, W1, Dl), BF),
            V((QC, Dl), BF),
            V((Dl, FT * HD), BF),
            V((Dl, FT * HD), BF),
            V(key_cache.shape, BF),
            V(value_cache.shape, BF),
            V((O, S, G3 + HD), BF),
            V((T, n, S, G3 + HD), BF),
            V((T, S, QG), BF),
            V((T, S, 2 * HD), BF),
            V((T, S, HD), F32),
            V((O, S, QG), BF),
            V((O, S, 2 * HD), BF),
            V((O, S, QG + HD), BF),
            V((T, n, S, QG + HD), BF),
            V((T, S, QG), BF),
            V((O, S, QG), BF),
            V((T, S, Dl), F32),
            V((O, S, 2 * W0 + HD), BF),
            V((O, S, 2 * W1), BF),
            V((T, n, S, 2 * W0 + HD), BF),
            V((T, n, S, 2 * W1), BF),
            V((T, S, W0), BF),
            V((T, S, W1), BF),
            V((O, S, W0), BF),
            V((O, S, W1), BF),
            V((T, S, Dl), F32),
            dma((5,)),
            dma((5,)),
            dma((O, 2, 3)),
            dma((2, O)),
            dma((O,)),
            dma((T, n)),
            dma((T, n)),
            dma((O,)),
            dma((T, n)),
            dma((O,)),
            dma((O,)),
            dma((T, n)),
            dma((T, n)),
            dma((O,)),
            dma((T,)),
            dma((T,)),
            dma((O, 2)),
            dma((T, n, 2)),
            dma((2, T, n)),
            dma((O, 2)),
            dma((T,)),
            dma((T,)),
        ],
        compiler_params=pltpu.CompilerParams(
            collective_id=0, has_side_effects=True, vmem_limit_bytes=67000000
        ),
    )(
        lengths,
        hidden,
        gain_in[None, :],
        gain_post[None, :],
        freq,
        key_cache,
        value_cache,
        w_query,
        w_key,
        w_value,
        w_output,
        w_gate,
        w_up,
        w_down,
    )
    return pl.pallas_call(
        split_kernel,
        out_shape=(
            jax.ShapeDtypeStruct((S, Dl), BF),
            jax.ShapeDtypeStruct((S, KC), BF),
            jax.ShapeDtypeStruct((S, KC), BF),
        ),
        in_specs=[vmem],
        out_specs=(vmem,) * 3,
    )(packed)


def solution(mesh):
    placed = (
        P("groups", "kvseq"),
        P("groups"),
        P("groups", "kvseq", "tensor"),
        P("groups", "kvseq", "tensor"),
        P("kvseq"),
        P("kvseq", "tensor"),
        P("kvseq", "tensor"),
        P("kvseq", "tensor"),
        P("tensor", "kvseq"),
        P("kvseq"),
        P("kvseq", "tensor"),
        P("kvseq", "tensor"),
        P("tensor", "kvseq"),
    )
    return jax.shard_map(
        functools.partial(per_device, mesh.shape["kvseq"], mesh.shape["tensor"]),
        mesh=mesh,
        in_specs=placed,
        out_specs=(P("groups", "kvseq"), P("groups", "tensor"), P("groups", "tensor")),
        check_vma=False,
    )
```

time: 51.9 us -> 44.2 us (0.85)
  Pallas kernels: 51 us -> 43.4 us
    pallas_call x1, Pallas kernels: 49.6 us -> 42 us  [per_device(): pl.pallas_call(functools.partial(layer_kernel, c), out_shape=jax.ShapeDty...]
where the time goes in v1:
time: 44.2 us; the launch traced here: 44 us
  Pallas kernels  43.4 us (98%)
  between operations  0.64 us (1%)
    pallas_call x1, Pallas kernels, per_device(): pl.pallas_call(functools.partial(layer_kernel, c), out_shape=jax.ShapeDty...  42 us
    pallas_call x1, Pallas kernels, per_device(): pl.pallas_call(split_kernel, out_shape=(jax.ShapeDtypeStruct((S, Dl), BF)...  1.37 us

profile of v1, /device:TPU:0, one launch (start us, length us, event | category | flops | bytes accessed | tf_op | source)
XLA Modules:
  0.0 44.0 jit_solution(6044961662362375289)
XLA Ops:
  0.6 42.0 %shard_map.157.packed = bf16[8,2048]{1,0:T(8,128)(2,1)} custom-call(s32[8]{0:T(128)} %lengths_hbm.1, bf16[8,1024]{1,0:T(8,128)(2,1)} %hidden_hbm.1, f32[1,1024]{1,0:T(1,128)} %bitcast.2, f32[1,1024]{1,0:T(1,128)} %bitcast.3, f32[1,128]{1,0:T(1,128)} %constant.2.clone.freq_hbm, bf16[8,256,512]{2,1,0:T(8,128)(2,1)} %kc_hbm.1, bf16[8,256,512]{2,1,0:T(8,128)(2,1)} %vc_hbm.1, ...), custom_call_target="tpu_custom_call" | custom-call | tf_op jit(solution)/shard_map/pallas_call | solution.py:618
  42.7 1.4 %shard_map.158 = (bf16[8,1024]{1,0:T(8,128)(2,1)}, bf16[8,512]{1,0:T(8,128)(2,1)}, bf16[8,512]{1,0:T(8,128)(2,1)}) custom-call(bf16[8,2048]{1,0:T(8,128)(2,1)} %shard_map.157.packed), custom_call_target="tpu_custom_call" | custom-call | tf_op jit(solution)/shard_map/pallas_call | solution.py:699

commit v2 on v1

--- a/solution.py
+++ b/solution.py
@@ -163,16 +163,23 @@
                 local(
                     src.at[pl.ds(b * half, half), pl.ds(mult(o * width, HD), width)],
                     wqkv.at[k, pl.ds(b * half, half), pl.ds(at, width)],
-                    fsem.at[k, b, i],
+                    fsem.at[k, b],
                 )
-                for i, (src, at, width) in enumerate(
-                    ((wq_hbm, 0, QG), (wk_hbm, QG, HD), (wv_hbm, QG + HD, HD))
+                for src, at, width in (
+                    (wq_hbm, 0, QG),
+                    (wk_hbm, QG, HD),
+                    (wv_hbm, QG + HD, HD),
                 )
             ]
             for b in range(2)
         ]
 
     firsts = [first(k) for k in range(O)]
+
+    def first_wait(k, b):
+        rows = pl.ds(b * half, half)
+        local(wq_hbm.at[rows, pl.ds(0, G3)], wqkv.at[k, rows, :], fsem.at[k, b]).wait()
+
     kv_copies = [local(kc_hbm, kc, wsem.at[0]), local(vc_hbm, vc, wsem.at[1])]
     later = [
         local(wo_hbm, wo, wsem.at[2]),
@@ -187,10 +194,10 @@
         return wqkv.at[o, pl.ds(0, W1), pl.ds(0, Dl)] if c["reuse"] else tail.at[o]
 
     downs_0 = [
-        local(wd_hbm.at[pl.ds(o * FO * HD, W0), :], down_0(o), dsem.at[0, o]) for o in range(O)
+        local(wd_hbm.at[pl.ds(o * FO * HD, W0), :], down_0(o), dsem.at[0]) for o in range(O)
     ]
     downs_1 = [
-        local(wd_hbm.at[pl.ds((o * FO + F0) * HD, W1), :], down_1(o), dsem.at[1, o])
+        local(wd_hbm.at[pl.ds((o * FO + F0) * HD, W1), :], down_1(o), dsem.at[1])
         for o in range(O)
     ]
     for x in small:
@@ -232,23 +239,22 @@
         def _():
             dst[...] = src[...]
 
-    def scatter_wait_send(src, dst, s_sem, r_sem, o):
-        @pl.when(jnp.logical_not(mine(o)))
+    def scatter_wait_send(send, s_sem):
+        @pl.when(jnp.logical_not(owner))
         def _():
-            to_owner(src, dst, s_sem, r_sem, o).wait_send()
-
-    def owner_wait(recv, s_sem, r_sem, tt):
-        def one(k, _):
-            def wait():
-                remote(recv(k), recv(k), s_sem, r_sem(k), k, tt).wait_recv()
-
-            if tt == T - 1:
-                pl.when(k != me)(wait)
-            else:
-                wait()
-            return 0
-
-        lax.fori_loop(0, n, one, 0)
+            remote(send, send, s_sem, s_sem, me, t).wait_send()
+
+        @pl.when(owner)
+        def _():
+            x = send.at[pl.ds(0, O - 1)]
+            remote(x, x, s_sem, s_sem, me, t).wait_send()
+
+    def arrivals(tt):
+        return pl.ds(0, n - 1 if tt == T - 1 else n)
+
+    def owner_wait(recv, r_sem, tt):
+        x = recv.at[tt, arrivals(tt)]
+        remote(x, x, sa_s, r_sem, me, tt).wait_recv()
 
     def each_target(f):
         def cross(k, _):
@@ -262,41 +268,37 @@
         lax.fori_loop(0, half_n, cross, 0)
         lax.fori_loop(0, n - half_n, same, 0)
 
-    def spread(src, dst, s_sem, r_sem, tt):
+    def spread(src, dst, s_sem, r_sem, tt, rising=False):
         def one(d):
             def send():
-                remote(src, dst, s_sem.at[tt, d], r_sem, d, tt).start()
+                remote(src, dst, s_sem.at[tt], r_sem, d, tt).start()
 
             if tt == T - 1:
                 pl.when(d != me)(send)
             else:
                 send()
 
-        each_target(one)
+        if rising:
+            lax.fori_loop(0, n, lambda d, _: (one(d), 0)[1], 0)
+        else:
+            each_target(one)
         if tt == T - 1:
             dst[...] = src[...]
 
-    def spread_wait_send(src, dst, s_sem, r_sem, tt):
-        def one(d, _):
-            def wait():
-                remote(src, dst, s_sem.at[tt, d], r_sem, d, tt).wait_send()
-
-            if tt == T - 1:
-                pl.when(d != me)(wait)
-            else:
-                wait()
-            return 0
-
-        lax.fori_loop(0, n, one, 0)
+    def spread_wait_send(like, width, s_sem, tt):
+        x = like.at[tt, arrivals(tt), :, pl.ds(0, width)]
+        remote(x, x, s_sem.at[tt], s_sem.at[tt], me, tt).wait_send()
 
     def spread_wait(dst, s_sem, r_sem, o):
         @pl.when(jnp.logical_not(mine(o)))
         def _():
-            remote(dst, dst, s_sem.at[0, 0], r_sem, base + o, T - 1).wait_recv()
+            remote(dst, dst, s_sem.at[0], r_sem, base + o, T - 1).wait_recv()
 
     def pair_copies(part, s_sem, r_sem):
         return [
-            remote(part.at[t], part.at[t], s_sem.at[k], r_sem.at[t], me, lax.rem(t + k, T))
+            remote(
+                part.at[t], part.at[t], s_sem.at[k - 1], r_sem.at[k - 1], me, lax.rem(t + k, T)
+            )
             for k in range(1, T)
         ]
 
@@ -304,8 +306,9 @@
         for x in pair_copies(part, s_sem, r_sem):
             x.start()
         for k in range(1, T):
-            src = lax.rem(t + k, T)
-            remote(part.at[src], part.at[src], s_sem.at[k], r_sem.at[src], me, src).wait_recv()
+            src = lax.rem(t + T - k, T)
+            x = part.at[src]
+            remote(x, x, s_sem.at[k - 1], r_sem.at[k - 1], me, src).wait_recv()
         total = part[0]
         for i in range(1, T):
             total = total + part[i]
@@ -331,11 +334,9 @@
 
     for k in range(O):
         o = order(k)
-        for x in firsts[k][0]:
-            x.wait()
+        first_wait(k, 0)
         part = jnp.dot(xg[:, :half], wqkv[k, :half, :], preferred_element_type=F32)
-        for x in firsts[k][1]:
-            x.wait()
+        first_wait(k, 1)
         if k == max(O - 2, 0):
             for x in kv_copies:
                 x.start(priority=1)
@@ -344,7 +345,7 @@
         send_a[k, :, G3:] = sq
         if k == 0:
             pl.semaphore_wait(barrier, n * T - 1)
-        scatter(send_a.at[k], recv_a.at[t, me], sa_s.at[k], sa_r.at[t, me], o)
+        scatter(send_a.at[k], recv_a.at[t, me], sa_s, sa_r.at[t], o)
     for x in later + downs_1:
         x.start(priority=1)
 
@@ -362,7 +363,7 @@
     @pl.when(owner)
     def _():
         for tt in reversed(range(T)):
-            owner_wait(lambda k: recv_a.at[tt, k], sa_s.at[0], lambda k: sa_r.at[tt, k], tt)
+            owner_wait(recv_a, sa_r.at[tt], tt)
             total = accumulate(n, lambda k: recv_a[tt, k].astype(F32))
             scale = row_scale(total[:, G3:])
             for j in range(PG + 1):
@@ -375,7 +376,7 @@
             kvg[tt, :, HD:] = (total[:, QG + HD : G3] * scale).astype(BF)
             spread(qg.at[tt], all_q.at[o_me], ga_s, ga_r.at[o_me], tt)
         for tt in range(T):
-            spread(kvg.at[tt], all_kv.at[o_me], gk_s, gk_r.at[o_me], tt)
+            spread(kvg.at[tt], all_kv.at[o_me], gk_s, gk_r, tt)
         for tt in range(T):
             key = kvg[tt, :, :HD].astype(F32)
             block = jnp.zeros((S, HD), F32)
@@ -399,9 +400,7 @@
     group = lane % 16
     third = (lane % (HD // 2)) // 16
 
-    def attend(i, _):
-        g = near(i)
-        spread_wait(all_q.at[g], ga_s, ga_r.at[g], g)
+    def attend_one(g):
         q = jnp.concatenate(
             [all_q[g, :, j * HD : (j + 1) * HD].astype(F32) for j in range(PG)], axis=0
         ).astype(BF)
@@ -432,15 +431,25 @@
         low = rest - middle
         parts = jnp.where(third == 0, high, jnp.where(third == 1, middle, low))
         send_b[g, :, QG:] = parts.astype(BF)
-        scatter(send_b.at[g], recv_b.at[t, me], sb_s.at[g], sb_r.at[t, me], g)
+
+    step = 1
+
+    def attend(i, _):
+        blocks = [near(i * step + j) for j in range(step)]
+        for g in blocks:
+            spread_wait(all_q.at[g], ga_s, ga_r.at[g], g)
+        for g in blocks:
+            attend_one(g)
+        for g in blocks:
+            scatter(send_b.at[g], recv_b.at[t, me], sb_s, sb_r.at[t], g)
         return 0
 
-    lax.fori_loop(0, O, attend, 0)
+    lax.fori_loop(0, O // step, attend, 0)
 
     @pl.when(owner)
     def _():
         for tt in reversed(range(T)):
-            owner_wait(lambda k: recv_b.at[tt, k], sb_s.at[0], lambda k: sb_r.at[tt, k], tt)
+            owner_wait(recv_b, sb_r.at[tt], tt)
 
             def stats(k):
                 x = recv_b[tt, k, :, QG:].astype(F32)
@@ -506,13 +515,21 @@
                     send[o, :, b * W + j : b * W + j + step] = x.astype(BF)
             if i == 0:
                 send[o, :, 2 * W :] = sq_post
-            scatter(send.at[o], recv.at[t, me], sc_s.at[o, i], sc_r.at[t, me, i], o)
+            scatter(send.at[o], recv.at[t, me], sc_s.at[i], sc_r.at[t, i], o)
         return 0
 
     lax.fori_loop(0, O, widen, 0)
 
+    @pl.when(jnp.logical_not(owner))
+    def _():
+        remote(all_kv, all_kv, gk_s.at[0], gk_r, me, t).wait_recv()
+
+    @pl.when(owner)
+    def _():
+        x = all_kv.at[pl.ds(0, O - 1)]
+        remote(x, x, gk_s.at[0], gk_r, me, t).wait_recv()
+
     for g in range(O):
-        spread_wait(all_kv.at[g], gk_s, gk_r.at[g], g)
         out[:, Dl + g * HD : Dl + (g + 1) * HD] = all_kv[g, :, :HD]
         out[:, Dl + KC + g * HD : Dl + KC + (g + 1) * HD] = all_kv[g, :, HD:]
 
@@ -521,9 +538,7 @@
         scales = [None] * T
         for i, recv, ic, all_c, W in ((0, recv_c0, ic0, all_c0, W0), (1, recv_c1, ic1, all_c1, W1)):
             for tt in reversed(range(T)):
-                owner_wait(
-                    lambda k: recv.at[tt, k], sc_s.at[0, 0], lambda k: sc_r.at[tt, k, i], tt
-                )
+                owner_wait(recv, sc_r.at[tt, i], tt)
                 if i == 0:
                     scales[tt] = row_scale(
                         accumulate(n, lambda k: recv[tt, k, :, 2 * W :].astype(F32))
@@ -534,10 +549,11 @@
                     gate = gate * scales[tt]
                     up = up * scales[tt]
                     ic[tt, :, j : j + HD] = (gate * jax.nn.sigmoid(gate) * up).astype(BF)
-                spread(ic.at[tt], all_c.at[o_me], gc_s.at[i], gc_r.at[o_me, i], tt)
-
-    for x in downs_0 + downs_1:
-        x.wait()
+                spread(ic.at[tt], all_c.at[o_me], gc_s.at[i], gc_r.at[o_me, i], tt, rising=True)
+
+    for i, W in ((0, W0), (1, W1)):
+        rows = pl.ds(0, O * W)
+        local(wd_hbm.at[rows, :], wo.at[rows, :], dsem.at[i]).wait()
 
     def down_block(k, acc):
         o = near(k)
@@ -549,27 +565,22 @@
     part_2[t] = lax.fori_loop(0, O, down_block, jnp.zeros((S, Dl), F32))
     out[:, :Dl] = (residual + pair_sum(part_2, t2_s, t2_r)).astype(BF)
 
-    for k in range(O):
-        scatter_wait_send(send_a.at[k], recv_a.at[t, me], sa_s.at[k], sa_r.at[t, me], order(k))
-
-    def sent(o, _):
-        scatter_wait_send(send_b.at[o], recv_b.at[t, me], sb_s.at[o], sb_r.at[t, me], o)
-        for i, send, recv in ((0, send_c0, recv_c0), (1, send_c1, recv_c1)):
-            scatter_wait_send(
-                send.at[o], recv.at[t, me], sc_s.at[o, i], sc_r.at[t, me, i], o
-            )
-        return 0
-
-    lax.fori_loop(0, O, sent, 0)
+    for send, s_sem in (
+        (send_a, sa_s),
+        (send_b, sb_s),
+        (send_c0, sc_s.at[0]),
+        (send_c1, sc_s.at[1]),
+    ):
+        scatter_wait_send(send, s_sem)
 
     @pl.when(owner)
     def _():
         for tt in range(T):
-            spread_wait_send(qg.at[tt], all_q.at[o_me], ga_s, ga_r.at[o_me], tt)
-            spread_wait_send(kvg.at[tt], all_kv.at[o_me], gk_s, gk_r.at[o_me], tt)
-            spread_wait_send(ab.at[tt], all_b.at[o_me], gb_s, gb_r.at[o_me], tt)
-            spread_wait_send(ic0.at[tt], all_c0.at[o_me], gc_s.at[0], gc_r.at[o_me, 0], tt)
-            spread_wait_send(ic1.at[tt], all_c1.at[o_me], gc_s.at[1], gc_r.at[o_me, 1], tt)
+            spread_wait_send(recv_b, QG, ga_s, tt)
+            spread_wait_send(recv_b, 2 * HD, gk_s, tt)
+            spread_wait_send(recv_b, QG, gb_s, tt)
+            spread_wait_send(recv_c0, W0, gc_s.at[0], tt)
+            spread_wait_send(recv_c1, W1, gc_s.at[1], tt)
 
     for part, s_sem, r_sem in ((part_1, t1_s, t1_r), (part_2, t2_s, t2_r)):
         for x in pair_copies(part, s_sem, r_sem):
@@ -606,7 +617,7 @@
     QG = PG * HD
     G3 = QG + 2 * HD
     W0, W1 = F0 * HD, F1 * HD
-    assert W0 <= QG
+    assert W1 <= QG
     reuse = W1 <= Dl <= G3
     c = dict(n=n, T=T, O=O, S=S, Dl=Dl, L=L, PG=PG, FO=FO, F0=F0, F1=F1, reuse=reuse)
     half = np.arange(HD) % (HD // 2)
@@ -617,7 +628,7 @@
     vmem = pl.BlockSpec(memory_space=pltpu.VMEM)
     packed = pl.pallas_call(
         functools.partial(layer_kernel, c),
-        out_shape=jax.ShapeDtypeStruct((S, Dl + 2 * KC), BF),
+        out_shape=pltpu.VMEM((S, Dl + 2 * KC), BF),
         in_specs=[anywhere] * 14,
         out_specs=vmem,
         scratch_shapes=[
@@ -656,26 +667,26 @@
             V((T, S, Dl), F32),
             dma((5,)),
             dma((5,)),
-            dma((O, 2, 3)),
-            dma((2, O)),
-            dma((O,)),
-            dma((T, n)),
-            dma((T, n)),
-            dma((O,)),
-            dma((T, n)),
-            dma((O,)),
-            dma((O,)),
-            dma((T, n)),
-            dma((T, n)),
+            dma((O, 2)),
+            dma((2,)),
+            dma,
+            dma((T,)),
+            dma((T,)),
             dma((O,)),
             dma((T,)),
-            dma((T,)),
-            dma((O, 2)),
-            dma((T, n, 2)),
-            dma((2, T, n)),
-            dma((O, 2)),
+            dma,
+            dma,
             dma((T,)),
             dma((T,)),
+            dma((O,)),
+            dma((T - 1,)),
+            dma((T - 1,)),
+            dma((2,)),
+            dma((T, 2)),
+            dma((2, T)),
+            dma((O, 2)),
+            dma((T - 1,)),
+            dma((T - 1,)),
         ],
         compiler_params=pltpu.CompilerParams(
             collective_id=0, has_side_effects=True, vmem_limit_bytes=67000000
@@ -705,7 +716,7 @@
         ),
         in_specs=[vmem],
         out_specs=(vmem,) * 3,
-    )(packed)
+    )(pltpu.with_memory_space_constraint(packed, pltpu.VMEM))
 
 
 def solution(mesh):

time: 44.2 us -> 41.2 us (0.932)
  Pallas kernels: 43.4 us -> 40.4 us
    pallas_call x1, Pallas kernels: 42 us -> 39.8 us  [per_device(): pl.pallas_call(functools.partial(layer_kernel, c), out_shape=pltpu.VMEM((...]
    pallas_call x1, Pallas kernels: 1.37 us -> 0.61 us  [per_device(): pl.pallas_call(split_kernel, out_shape=(jax.ShapeDtypeStruct((S, Dl), BF)...]
where the time goes in v2:
time: 41.2 us; the launch traced here: 41.1 us
  Pallas kernels  40.4 us (98%)
  between operations  0.64 us (2%)
    pallas_call x1, Pallas kernels, per_device(): pl.pallas_call(functools.partial(layer_kernel, c), out_shape=pltpu.VMEM((...  39.8 us

profile of v2, /device:TPU:0, one launch (start us, length us, event | category | flops | bytes accessed | tf_op | source)
XLA Modules:
  0.0 41.1 jit_solution(15055087669499912676)
XLA Ops:
  0.6 39.8 %shard_map.157.packed = bf16[8,2048]{1,0:T(8,128)(2,1)S(1)} custom-call(s32[8]{0:T(128)} %lengths_hbm.1, bf16[8,1024]{1,0:T(8,128)(2,1)} %hidden_hbm.1, f32[1,1024]{1,0:T(1,128)} %bitcast.2, f32[1,1024]{1,0:T(1,128)} %bitcast.3, f32[1,128]{1,0:T(1,128)} %constant.2.clone.freq_hbm, bf16[8,256,512]{2,1,0:T(8,128)(2,1)} %kc_hbm.1, bf16[8,256,512]{2,1,0:T(8,128)(2,1)} %vc_hbm.1, ...), custom_call_target="tpu_custom_call" | custom-call | tf_op jit(solution)/shard_map/pallas_call | solution.py:629
  40.5 0.6 %shard_map.158 = (bf16[8,1024]{1,0:T(8,128)(2,1)}, bf16[8,512]{1,0:T(8,128)(2,1)}, bf16[8,512]{1,0:T(8,128)(2,1)}) custom-call(bf16[8,2048]{1,0:T(8,128)(2,1)S(1)} %shard_map.157.packed), custom_call_target="tpu_custom_call" | custom-call | tf_op jit(solution)/shard_map/pallas_call | solution.py:710

commit v3 on v2

--- a/solution.py
+++ b/solution.py
@@ -10,6 +10,7 @@
 
 HD = 128
 epsilon = 1e-06
+ATTEND_ORDER = (0, 3, 2, 1)
 rope_base = 1000000.0
 BF = jnp.bfloat16
 F32 = jnp.float32
@@ -362,13 +363,15 @@
 
     @pl.when(owner)
     def _():
+        scale = None
         for tt in reversed(range(T)):
             owner_wait(recv_a, sa_r.at[tt], tt)
             total = accumulate(n, lambda k: recv_a[tt, k].astype(F32))
-            scale = row_scale(total[:, G3:])
+            if scale is None:
+                scale = row_scale(total[:, G3:])
             for j in range(PG + 1):
-                v = total[:, j * HD : (j + 1) * HD] * scale
-                v = (v * cosine + pltpu.roll(v, HD // 2, 1) * sine).astype(BF)
+                v = total[:, j * HD : (j + 1) * HD]
+                v = ((v * cosine + pltpu.roll(v, HD // 2, 1) * sine) * scale).astype(BF)
                 if j < PG:
                     qg[tt, :, j * HD : (j + 1) * HD] = v
                 else:
@@ -432,19 +435,18 @@
         parts = jnp.where(third == 0, high, jnp.where(third == 1, middle, low))
         send_b[g, :, QG:] = parts.astype(BF)
 
-    step = 1
-
     def attend(i, _):
-        blocks = [near(i * step + j) for j in range(step)]
-        for g in blocks:
-            spread_wait(all_q.at[g], ga_s, ga_r.at[g], g)
-        for g in blocks:
-            attend_one(g)
-        for g in blocks:
-            scatter(send_b.at[g], recv_b.at[t, me], sb_s, sb_r.at[t], g)
+        k = i
+        if O == len(ATTEND_ORDER):
+            for j, v in enumerate(ATTEND_ORDER):
+                k = jnp.where(i == j, v, k)
+        g = near(k)
+        spread_wait(all_q.at[g], ga_s, ga_r.at[g], g)
+        attend_one(g)
+        scatter(send_b.at[g], recv_b.at[t, me], sb_s, sb_r.at[t], g)
         return 0
 
-    lax.fori_loop(0, O // step, attend, 0)
+    lax.fori_loop(0, O, attend, 0)
 
     @pl.when(owner)
     def _():
@@ -455,6 +457,9 @@
                 x = recv_b[tt, k, :, QG:].astype(F32)
                 return x + pltpu.roll(x, HD - 16, 1) + pltpu.roll(x, HD - 32, 1)
 
+            if n <= 8:
+                known = [stats(k) for k in range(n)]
+                stats = known.__getitem__
             top = accumulate(n, stats, jnp.maximum)
             total = accumulate(
                 n, lambda k: pltpu.roll(stats(k), HD // 2, 1) * jnp.exp(stats(k) - top)

time: 41.2 us -> 40.4 us (0.981)
  Pallas kernels: 40.4 us -> 39.6 us
    pallas_call x1, Pallas kernels: 39.8 us -> 39 us  [per_device(): pl.pallas_call(functools.partial(layer_kernel, c), out_shape=pltpu.VMEM((...]
where the time goes in v3:
time: 40.4 us; the launch traced here: 40.2 us
  Pallas kernels  39.6 us (98%)
  between operations  0.64 us (2%)
    pallas_call x1, Pallas kernels, per_device(): pl.pallas_call(functools.partial(layer_kernel, c), out_shape=pltpu.VMEM((...  39 us

profile of v3, /device:TPU:0, one launch (start us, length us, event | category | flops | bytes accessed | tf_op | source)
XLA Modules:
  0.0 40.2 jit_solution(3680971556909317223)
XLA Ops:
  0.6 39.0 %shard_map.157.packed = bf16[8,2048]{1,0:T(8,128)(2,1)S(1)} custom-call(s32[8]{0:T(128)} %lengths_hbm.1, bf16[8,1024]{1,0:T(8,128)(2,1)} %hidden_hbm.1, f32[1,1024]{1,0:T(1,128)} %bitcast.2, f32[1,1024]{1,0:T(1,128)} %bitcast.3, f32[1,128]{1,0:T(1,128)} %constant.2.clone.freq_hbm, bf16[8,256,512]{2,1,0:T(8,128)(2,1)} %kc_hbm.1, bf16[8,256,512]{2,1,0:T(8,128)(2,1)} %vc_hbm.1, ...), custom_call_target="tpu_custom_call" | custom-call | tf_op jit(solution)/shard_map/pallas_call | solution.py:634
  39.6 0.6 %shard_map.158 = (bf16[8,1024]{1,0:T(8,128)(2,1)}, bf16[8,512]{1,0:T(8,128)(2,1)}, bf16[8,512]{1,0:T(8,128)(2,1)}) custom-call(bf16[8,2048]{1,0:T(8,128)(2,1)S(1)} %shard_map.157.packed), custom_call_target="tpu_custom_call" | custom-call | tf_op jit(solution)/shard_map/pallas_call | solution.py:715

commit v4 on v3

--- a/solution.py
+++ b/solution.py
@@ -379,8 +379,6 @@
             kvg[tt, :, HD:] = (total[:, QG + HD : G3] * scale).astype(BF)
             spread(qg.at[tt], all_q.at[o_me], ga_s, ga_r.at[o_me], tt)
         for tt in range(T):
-            spread(kvg.at[tt], all_kv.at[o_me], gk_s, gk_r, tt)
-        for tt in range(T):
             key = kvg[tt, :, :HD].astype(F32)
             block = jnp.zeros((S, HD), F32)
             for j in range(PG):
@@ -485,6 +483,8 @@
                 res = mixed[j] + own_weight[:, j : j + 1] * val
                 ab[tt, :, j * HD : (j + 1) * HD] = res.astype(BF)
             spread(ab.at[tt], all_b.at[o_me], gb_s, gb_r.at[o_me], tt)
+        for tt in range(T):
+            spread(kvg.at[tt], all_kv.at[o_me], gk_s, gk_r, tt)
 
     later[0].wait()
 
@@ -542,7 +542,7 @@
     def _():
         scales = [None] * T
         for i, recv, ic, all_c, W in ((0, recv_c0, ic0, all_c0, W0), (1, recv_c1, ic1, all_c1, W1)):
-            for tt in reversed(range(T)):
+            for tt in range(T):
                 owner_wait(recv, sc_r.at[tt, i], tt)
                 if i == 0:
                     scales[tt] = row_scale(

time: 40.4 us -> 39.9 us (0.988)
  Pallas kernels: 39.6 us -> 39.1 us
    pallas_call x1, Pallas kernels: 39 us -> 38.5 us  [per_device(): pl.pallas_call(functools.partial(layer_kernel, c), out_shape=pltpu.VMEM((...]
where the time goes in v4:
time: 39.9 us; the launch traced here: 39.8 us
  Pallas kernels  39.1 us (98%)
  between operations  0.64 us (2%)
    pallas_call x1, Pallas kernels, per_device(): pl.pallas_call(functools.partial(layer_kernel, c), out_shape=pltpu.VMEM((...  38.5 us

profile of v4, /device:TPU:0, one launch (start us, length us, event | category | flops | bytes accessed | tf_op | source)
XLA Modules:
  0.0 39.8 jit_solution(9120253145339117429)
XLA Ops:
  0.6 38.5 %shard_map.157.packed = bf16[8,2048]{1,0:T(8,128)(2,1)S(1)} custom-call(s32[8]{0:T(128)} %lengths_hbm.1, bf16[8,1024]{1,0:T(8,128)(2,1)} %hidden_hbm.1, f32[1,1024]{1,0:T(1,128)} %bitcast.2, f32[1,1024]{1,0:T(1,128)} %bitcast.3, f32[1,128]{1,0:T(1,128)} %constant.2.clone.freq_hbm, bf16[8,256,512]{2,1,0:T(8,128)(2,1)} %kc_hbm.1, bf16[8,256,512]{2,1,0:T(8,128)(2,1)} %vc_hbm.1, ...), custom_call_target="tpu_custom_call" | custom-call | tf_op jit(solution)/shard_map/pallas_call | solution.py:634
  39.2 0.6 %shard_map.158 = (bf16[8,1024]{1,0:T(8,128)(2,1)}, bf16[8,512]{1,0:T(8,128)(2,1)}, bf16[8,512]{1,0:T(8,128)(2,1)}) custom-call(bf16[8,2048]{1,0:T(8,128)(2,1)S(1)} %shard_map.157.packed), custom_call_target="tpu_custom_call" | custom-call | tf_op jit(solution)/shard_map/pallas_call | solution.py:715
